TPU v7x, 256 devices: a whole 4x4x8 slice. The times are simulated.
256 devices in a mesh: row: 8 (over y, x_lo), col: 32 (over z, x_hi, core).
Axes of the slice: x: 4 (x_hi: 2, x_lo: 2; x = x_hi * 2 + x_lo), y: 4, z: 8, core: 2. Of those that a mesh axis runs over, the one named last changes fastest.
Arguments:
- density: bfloat16 [8192, 8192], P('row', 'col'), may hold values from -0.0625 to 0.0625
- density_mask: int32 [64, 64], P('row', 'col'), may hold values from 0 to 1, as said below
- response: bfloat16 [2, 8192, 8192], P(None, 'row', 'col'), may hold values from -6 to 6
- response_mask: int32 [2, 64, 64], P(None, 'row', 'col'), may hold values from 0 to 1, as said below
- filter_mask: int32 [64, 64], P('row', 'col'), may hold values from 0 to 1, as said below
Outputs:
- product: bfloat16 [2, 8192, 8192], P(None, 'row', 'col')
Inputs may be any that keep to these rules, and one draw needn't show every extreme that they name: `density_mask`: diagonal blocks are always nonzero; blocks within cyclic block distance 8 of the diagonal are more often nonzero than blocks further out; whole block rows and whole block columns may be nonzero. `response_mask`: for each direction, diagonal blocks are always nonzero; blocks within cyclic block distance 8 of the diagonal are more often nonzero than blocks further out; whole block rows and whole block columns may be nonzero. `filter_mask`: diagonal blocks are always kept; blocks within cyclic block distance 2 * 8 of the diagonal are more often kept than blocks further out; whole block rows and whole block columns may be kept.
All inputs are finite; a program needn't handle non-finite values.
Results may differ from a plain program's by a relative error of at most 0.001.
Values may be sent and summed in bfloat16 or wider, within the bound.
No kernel may reach another device: no remote copies, remote signals or barrier semaphores. Data moves between devices by JAX's collectives and lax.ppermute only.
A program may use at most 128 MiB of HBM per device.

v0:
```python
import jax
import jax.numpy as jnp
from jax import lax
from jax.sharding import PartitionSpec as P


def in_order(tiles, dim):
    dims = list(tiles.shape[1:])
    dims[dim] *= tiles.shape[0]
    return jnp.moveaxis(tiles, 0, dim).reshape(dims)


def sent_to_all(array, axis):
    peers = lax.axis_size(axis)
    return lax.all_to_all(
        jnp.broadcast_to(array[None], (peers, *array.shape)), axis, 0, 0, tiled=True
    )


def gather_directly(array, axis, dim):
    return in_order(sent_to_all(array, axis), dim)


def expand_blocks(values, mask, blocksize):
    lead = values.shape[:-2]
    height = values.shape[-2] // blocksize
    width = values.shape[-1] // blocksize
    shaped = values.reshape(lead + (height, blocksize, width, blocksize))
    scaled = shaped * mask.astype(values.dtype)[..., :, None, :, None]
    return scaled.reshape(values.shape)


def body(density, density_mask, response, response_mask, filter_mask):
    blocksize = density.shape[1] // density_mask.shape[1]
    masked_density = expand_blocks(density, density_mask, blocksize)
    masked_response = expand_blocks(response, response_mask, blocksize)
    density_full = lax.all_gather(masked_density, "col", axis=1, tiled=True)
    result = jnp.einsum(
        "ik,dkj->dij",
        density_full,
        gather_directly(masked_response, "row", 1),
        preferred_element_type=jnp.float32,
    )
    return expand_blocks(result, filter_mask, blocksize).astype(jnp.bfloat16)


def solution(mesh):
    in_specs = (
        P("row", "col"),
        P("row", "col"),
        P(None, "row", "col"),
        P(None, "row", "col"),
        P("row", "col"),
    )
    out_specs = P(None, "row", "col")
    return jax.shard_map(body, mesh=mesh, in_specs=in_specs, out_specs=out_specs, check_vma=False)
```

profile of v0, /device:TPU:1, one launch (start us, length us, event | category | flops | bytes accessed | tf_op | source)
XLA Modules:
  0.0 235.9 jit_solution(5093998022321355920)
XLA Ops:
  6.5 0.0 all-gather.2.cloned.1.call-start
  6.5 0.7 convert_element_type.13
  7.2 0.1 copy.13
  7.3 0.3 mul.39
  7.7 1.9 bitcast_multiply_fusion.1
  9.6 0.0 all-gather.2.cloned.1.call-update
  9.6 0.7 convert_element_type.12
  10.3 0.1 copy.10
  10.4 0.6 mul.36
  11.0 0.7 mul.37
  11.7 1.5 mul.38
  13.2 0.5 copy.11
  13.8 4.3 %broadcast_in_dim.2 = bf16[8,2,1024,256]{2,3,1,0:T(8,128)(2,1)} broadcast(bf16[2,1024,256]{1,2,0:T(8,128)(2,1)S(1)} %copy.11), dimensions={1,2,3} | broadcast | bytes 9437184 | tf_op jit(solution)/shard_map/broadcast_in_dim | solution.py:16
  18.1 0.0 copy-start
  18.1 6.1 %all-to-all-start = ((bf16[8,2,1024,256]{2,3,1,0:T(8,128)(2,1)}), bf16[8,2,1024,256]{2,3,1,0:T(8,128)(2,1)}, u32[]{:S(2)}, u32[]{:S(2)}) async-start(bf16[8,2,1024,256]{2,3,1,0:T(8,128)(2,1)} %broadcast_in_dim.2), calls=%async_computation | async-start | bytes 16777216 | tf_op jit(solution)/shard_map/all_to_all | solution.py:15
  24.1 0.0 copy-done
  24.1 0.1 mul.42
  24.3 0.2 copy.20
  24.5 136.0 %all-to-all-done = bf16[8,2,1024,256]{2,3,1,0:T(8,128)(2,1)} async-done(((bf16[8,2,1024,256]{2,3,1,0:T(8,128)(2,1)}), bf16[8,2,1024,256]{2,3,1,0:T(8,128)(2,1)}, u32[]{:S(2)}, u32[]{:S(2)}) %all-to-all-start) | async-done | bytes 8388640 | tf_op jit(solution)/shard_map/all_to_all | solution.py:15
  160.5 8.0 %copy.15 = bf16[8,2,32,8,1024]{4,3,0,2,1:T(8,128)(2,1)} copy(bf16[8,2,32,8,1024]{4,3,2,1,0:T(8,128)(2,1)} %bitcast.3) | data formatting | bytes 16777216 | tf_op jit(solution)/shard_map/reshape | solution.py:10
  168.6 44.4 %all-gather.2.cloned.1.call-done = bf16[1024,8192]{1,0:T(8,128)(2,1)} async-done(((bf16[1024,256]{1,0:T(8,128)(2,1)}), bf16[1024,8192]{1,0:T(8,128)(2,1)}) %all-gather.2.cloned.1.call-update) | async-done | bytes 16777232 | tf_op jit(solution)/shard_map/all_gather | solution.py:37
  212.9 14.8 %fusion.2 = bf16[2,1024,256]{1,2,0:T(8,128)(2,1)S(1)} fusion(bf16[2,8192,256]{1,2,0:T(8,128)(2,1)} %bitcast.24, bf16[1024,8192]{1,0:T(8,128)(2,1)} %all-gather.2.cloned.1.call-done, f32[1024,256]{0,1:T(8,128)S(1)} %bitcast.27), kind=kOutput, calls=%fused_computation.3 | convolution fusion | flops 8590983168 | bytes 27262976 | tf_op jit(solution)/shard_map/ik,dkj->dij/dot_general | solution.py:38
  227.8 1.3 copy.14
  (1 shorter events, 0.0 us)
Async XLA Ops:
  6.5 206.4 %all-gather.2.cloned.1.call-start = ((), (), s32[]{:S(2)}) async-start(), calls=%async_computation.1 | async-start | bytes 17301504 | tf_op jit(solution)/shard_map/all_gather | solution.py:37
  18.1 6.1 %copy-start = (s32[8,2]{0,1:T(2,128)S(1)}, s32[8,2]{0,1:T(2,128)}, u32[]{:S(2)}) copy-start(s32[8,2]{0,1:T(2,128)} %param.9) | copy-start | bytes 196
  18.1 142.5 %all-to-all-start = ((bf16[8,2,1024,256]{2,3,1,0:T(8,128)(2,1)}), bf16[8,2,1024,256]{2,3,1,0:T(8,128)(2,1)}, u32[]{:S(2)}, u32[]{:S(2)}) async-start(bf16[8,2,1024,256]{2,3,1,0:T(8,128)(2,1)} %broadcast_in_dim.2), calls=%async_computation | async-start | bytes 16777216 | tf_op jit(solution)/shard_map/all_to_all | solution.py:15
Sparse Core Ops, SparseCore 0:
  9.9 202.9 all-gather.1
where the time goes:
time: 236 us
  waiting for transfers between devices  180 us (76%)
  local copies, waits for them, and re-layouts  16.4 us (7%)
  matrix products  14.8 us (6%)
  between operations  13.5 us (6%)
  starting transfers between devices  6.07 us (3%)
  other arithmetic  4.77 us (2%)
    all_to_all x1, waiting for transfers between devices, sent_to_all(): lax.all_to_all(jnp.broadcast_to(array[None], (peers, *array.shape)), axis...  136 us
    all_gather x1, waiting for transfers between devices, body(): density_full = lax.all_gather(masked_density, 'col', axis=1, tiled=True)  44.4 us
    dot_general x1, matrix products, body(): jnp.einsum('ik,dkj->dij', density_full, gather_directly(masked_response,...  14.8 us
    reshape x1, local copies, waits for them, and re-layouts, in_order(): return jnp.moveaxis(tiles, 0, dim).reshape(dims)  8.04 us
    all_to_all x1, starting transfers between devices, sent_to_all(): lax.all_to_all(jnp.broadcast_to(array[None], (peers, *array.shape)), axis...  6.07 us
  transfers between devices with their start and end apart: 2, of which 2 were waited for; matrix products, arithmetic and copies ran while one was open for 7% of the time, Pallas kernels for 0%

commit v1 on v0

--- a/solution.py
+++ b/solution.py
@@ -34,7 +34,8 @@
     blocksize = density.shape[1] // density_mask.shape[1]
     masked_density = expand_blocks(density, density_mask, blocksize)
     masked_response = expand_blocks(response, response_mask, blocksize)
-    density_full = lax.all_gather(masked_density, "col", axis=1, tiled=True)
+    stack = jnp.stack([masked_density] * lax.axis_size("col"))
+    density_full = jnp.concatenate(lax.all_to_all(stack, "col", 0, 0), axis=1)
     result = jnp.einsum(
         "ik,dkj->dij",
         density_full,

time: 236 us -> 553 us (2.34); the launches traced: 236 us -> 545 us
  waiting for transfers between devices: 180 us -> 442 us
  local copies, waits for them, and re-layouts: 16.4 us -> 65.8 us
  starting transfers between devices: 6.07 us -> 20 us
  between operations: 13.5 us -> 0.11 us
    all_to_all x0 -> x1, waiting for transfers between devices: none -> 350 us  [body(): density_full = jnp.concatenate(lax.all_to_all(stack, 'col', 0, 0), axis=1)]
    all_gather x1 -> x0, waiting for transfers between devices: 44.4 us -> none  [body(): density_full = lax.all_gather(masked_density, 'col', axis=1, tiled=True)]
    all_to_all x1, waiting for transfers between devices: 136 us -> 91.9 us  [sent_to_all(): lax.all_to_all(jnp.broadcast_to(array[None], (peers, *array.shape)), axis...]
    reshape x0 -> x2, local copies, waits for them, and re-layouts: none -> 43.5 us  [body(): density_full = jnp.concatenate(lax.all_to_all(stack, 'col', 0, 0), axis=1)]
    all_to_all x0 -> x1, starting transfers between devices: none -> 14 us  [body(): density_full = jnp.concatenate(lax.all_to_all(stack, 'col', 0, 0), axis=1)]
    another operation x0 -> x1, local copies, waits for them, and re-layouts: none -> 5.92 us  [body(): stack = jnp.stack([masked_density] * lax.axis_size('col'))]
  transfers between devices with their start and end apart: 2 -> 2, of which waited for: 2 -> 2; matrix products, arithmetic and copies ran while one was open for 7% -> 2% of each run, Pallas kernels for 0% -> 0%
where the time goes in v1:
time: 553 us; the launch traced here: 545 us
  waiting for transfers between devices  442 us (80%)
  local copies, waits for them, and re-layouts  65.8 us (12%)
  starting transfers between devices  20 us (4%)
  matrix products  14.8 us (3%)
    all_to_all x1, waiting for transfers between devices, body(): density_full = jnp.concatenate(lax.all_to_all(stack, 'col', 0, 0), axis=1)  350 us
    all_to_all x1, waiting for transfers between devices, sent_to_all(): lax.all_to_all(jnp.broadcast_to(array[None], (peers, *array.shape)), axis...  91.9 us
    reshape x2, local copies, waits for them, and re-layouts, body(): density_full = jnp.concatenate(lax.all_to_all(stack, 'col', 0, 0), axis=1)  43.5 us
    dot_general x1, matrix products, body(): jnp.einsum('ik,dkj->dij', density_full, gather_directly(masked_response,...  14.8 us
    all_to_all x1, starting transfers between devices, body(): density_full = jnp.concatenate(lax.all_to_all(stack, 'col', 0, 0), axis=1)  14 us
  transfers between devices with their start and end apart: 2, of which 2 were waited for; matrix products, arithmetic and copies ran while one was open for 2% of the time, Pallas kernels for 0%

profile of v1, /device:TPU:1, one launch (start us, length us, event | category | flops | bytes accessed | tf_op | source)
XLA Modules:
  0.0 545.1 jit_solution(1349697403112684294)
XLA Ops:
  0.0 0.7 convert_element_type.12
  0.7 0.1 copy.10
  0.8 0.6 mul.37
  1.4 0.7 mul.38
  2.1 1.5 mul.39
  3.6 0.5 copy.11
  4.2 4.3 broadcast_in_dim.2
  8.5 0.0 copy-start.2
  8.5 0.0 copy-start
  8.5 6.1 %all-to-all-start = ((bf16[8,2,1024,256]{2,3,1,0:T(8,128)(2,1)}), bf16[8,2,1024,256]{2,3,1,0:T(8,128)(2,1)}, u32[]{:S(2)}, u32[]{:S(2)}) async-start(bf16[8,2,1024,256]{2,3,1,0:T(8,128)(2,1)} %broadcast_in_dim.2), calls=%async_computation | async-start | bytes 16777216 | tf_op jit(solution)/shard_map/all_to_all | solution.py:15
  14.5 0.0 copy-done.2
  14.6 0.1 copy.13
  14.7 0.3 mul.40
  15.0 0.0 copy-done
  15.0 0.1 bitcast_multiply_fusion.1
  15.1 91.9 %all-to-all-done = bf16[8,2,1024,256]{2,3,1,0:T(8,128)(2,1)} async-done(((bf16[8,2,1024,256]{2,3,1,0:T(8,128)(2,1)}), bf16[8,2,1024,256]{2,3,1,0:T(8,128)(2,1)}, u32[]{:S(2)}, u32[]{:S(2)}) %all-to-all-start) | async-done | bytes 8388640 | tf_op jit(solution)/shard_map/all_to_all | solution.py:15
  107.0 5.9 %stack.3 = bf16[32,1024,256]{2,1,0:T(8,128)(2,1)} broadcast(bf16[1024,256]{1,0:T(8,128)(2,1)S(1)} %bitcast_multiply_fusion.1), dimensions={1,2} | broadcast | bytes 17301504 | tf_op jit(solution)/shard_map/stack | solution.py:37
  112.9 0.0 copy-start.1
  112.9 14.0 %all-to-all-start.1 = ((bf16[32,1024,256]{2,1,0:T(8,128)(2,1)}), bf16[32,1024,256]{2,1,0:T(8,128)(2,1)}, u32[]{:S(2)}, u32[]{:S(2)}) async-start(bf16[32,1024,256]{2,1,0:T(8,128)(2,1)} %stack.3), calls=%async_computation.1 | async-start | bytes 33554432 | tf_op jit(solution)/shard_map/all_to_all | solution.py:38
  126.9 0.0 copy-done.1
  126.9 0.1 mul.43
  127.1 0.2 copy.21
  127.3 8.0 %copy.16 = bf16[8,2,32,8,1024]{4,3,0,2,1:T(8,128)(2,1)} copy(bf16[8,2,32,8,1024]{4,3,2,1,0:T(8,128)(2,1)} %bitcast.3) | data formatting | bytes 16777216 | tf_op jit(solution)/shard_map/reshape | solution.py:10
  135.3 350.2 %all-to-all-done.1 = bf16[32,1024,256]{2,1,0:T(8,128)(2,1)} async-done(((bf16[32,1024,256]{2,1,0:T(8,128)(2,1)}), bf16[32,1024,256]{2,1,0:T(8,128)(2,1)}, u32[]{:S(2)}, u32[]{:S(2)}) %all-to-all-start.1) | async-done | bytes 16777248 | tf_op jit(solution)/shard_map/all_to_all | solution.py:38
  485.5 17.9 %copy.14 = bf16[1024,32,256]{2,1,0:T(8,128)(2,1)} copy(bf16[1024,32,256]{2,0,1:T(8,128)(2,1)} %bitcast.1) | data formatting | bytes 33554432 | tf_op jit(solution)/shard_map/reshape | solution.py:38
  503.4 25.6 %reshape.31 = bf16[1024,8192,1]{1,0,2:T(8,128)(2,1)} reshape(bf16[1024,32,256]{2,1,0:T(8,128)(2,1)} %copy.14) | data formatting | bytes 33554432 | tf_op jit(solution)/shard_map/reshape | solution.py:38
  529.0 14.8 %fusion = bf16[2,1024,256]{1,2,0:T(8,128)(2,1)S(1)} fusion(bf16[2,8192,256]{1,2,0:T(8,128)(2,1)} %bitcast.21, bf16[1024,8192,1]{1,0,2:T(8,128)(2,1)} %reshape.31, f32[1024,256]{0,1:T(8,128)S(1)} %bitcast.24), kind=kOutput, calls=%fused_computation.1 | convolution fusion | flops 8590983168 | bytes 27262976 | tf_op jit(solution)/shard_map/ik,dkj->dij/dot_general | solution.py:39
  543.8 1.3 copy.15
  (2 shorter events, 0.0 us)
Async XLA Ops:
  8.5 6.1 %copy-start.2 = (s32[8,2]{0,1:T(2,128)S(1)}, s32[8,2]{0,1:T(2,128)}, u32[]{:S(2)}) copy-start(s32[8,2]{0,1:T(2,128)} %param.6) | copy-start | bytes 196
  8.5 6.5 %copy-start = (bf16[1024,256]{1,0:T(8,128)(2,1)S(1)}, bf16[1024,256]{1,0:T(8,128)(2,1)}, u32[]{:S(2)}) copy-start(bf16[1024,256]{1,0:T(8,128)(2,1)} %param.5) | copy-start | bytes 1572868
  8.5 98.5 %all-to-all-start = ((bf16[8,2,1024,256]{2,3,1,0:T(8,128)(2,1)}), bf16[8,2,1024,256]{2,3,1,0:T(8,128)(2,1)}, u32[]{:S(2)}, u32[]{:S(2)}) async-start(bf16[8,2,1024,256]{2,3,1,0:T(8,128)(2,1)} %broadcast_in_dim.2), calls=%async_computation | async-start | bytes 16777216 | tf_op jit(solution)/shard_map/all_to_all | solution.py:15
  112.9 14.0 %copy-start.1 = (s32[8,2]{0,1:T(2,128)S(1)}, s32[8,2]{0,1:T(2,128)}, u32[]{:S(2)}) copy-start(s32[8,2]{0,1:T(2,128)} %param.9) | copy-start | bytes 196
  112.9 372.6 %all-to-all-start.1 = ((bf16[32,1024,256]{2,1,0:T(8,128)(2,1)}), bf16[32,1024,256]{2,1,0:T(8,128)(2,1)}, u32[]{:S(2)}, u32[]{:S(2)}) async-start(bf16[32,1024,256]{2,1,0:T(8,128)(2,1)} %stack.3), calls=%async_computation.1 | async-start | bytes 33554432 | tf_op jit(solution)/shard_map/all_to_all | solution.py:38
